TPU v7x, 32 devices: a whole 2x2x4 slice. The times are simulated.
32 devices in a mesh: section: 8 (over z, core), ep: 4 (over y, x).
Axes of the slice: x: 2, y: 2, z: 4, core: 2. Of those that a mesh axis runs over, the one named last changes fastest.
Arguments:
- states: bfloat16 [512, 3072], P(('section', 'ep')), may hold values from -6 to 6
- entering: bfloat16 [64, 3072], P('ep'), may hold values from -6 to 6
- seq_lens: int32 [9, 64], replicated, may hold values from 1 to 16, 512 in all within a row
- routes: int32 [8, 2, 64, 2], P('section', None, 'ep'), may hold values from 0 to 7, all different within a row; in each aligned block of 16 rows (0 to 15, 16 to 31, ..., all dimensions but the last counted through in order) at most 8 rows name the same one
- attn_norm: bfloat16 [8, 3072], P('section'), may hold values from 0.099609375 to 1.8984375
- ffn_norm: bfloat16 [8, 3072], P('section'), may hold values from 0.099609375 to 1.8984375
- wq: bfloat16 [8, 3072, 4096], P('section', None, 'ep'), may hold values from -0.109375 to 0.109375
- wk: bfloat16 [8, 3072, 1024], P('section', None, 'ep'), may hold values from -0.109375 to 0.109375
- wv: bfloat16 [8, 3072, 1024], P('section', None, 'ep'), may hold values from -0.109375 to 0.109375
- wo: bfloat16 [8, 4096, 3072], P('section', 'ep'), may hold values from -0.09375 to 0.09375
- router: bfloat16 [8, 3072, 8], P('section'), may hold values from -0.21875 to 0.21875
- w_gate: bfloat16 [8, 3072, 7168], P('section', None, 'ep'), may hold values from -0.109375 to 0.109375
- w_up: bfloat16 [8, 3072, 7168], P('section', None, 'ep'), may hold values from -0.109375 to 0.109375
- w_down: bfloat16 [8, 7168, 3072], P('section', 'ep'), may hold values from -0.125 to 0.125
- cache_k: bfloat16 [8, 2, 64, 8, 16, 128], P('section', None, 'ep'), may hold values from -127 to 127, as said below
- cache_v: bfloat16 [8, 2, 64, 8, 16, 128], P('section', None, 'ep'), may hold values from -127 to 127, as said below
- k_scale: float32 [8, 2, 64, 8, 4], P('section', None, 'ep'), may hold values from 0.004 to 2.4
- v_scale: float32 [8, 2, 64, 8, 4], P('section', None, 'ep'), may hold values from 0.004 to 0.04
Outputs:
- advanced: bfloat16 [512, 3072], P(('section', 'ep'))
Inputs may be any that keep to these rules, and one draw needn't show every extreme that they name: `seq_lens`: each row holds 64 lengths; the longest is exactly 16. `routes`: the two ids of a token differ. In the rows of one device (aligned blocks of 16 tokens of a section and step) no expert is named by more than 8 tokens. `cache_k`: whole numbers. `cache_v`: whole numbers.
All inputs are finite; a program needn't handle non-finite values.
Results may differ from a plain program's by a relative error of at most 0.033.
Values may be sent and summed in bfloat16 or wider, within the bound.
A program may use at most 128 MiB of HBM per device.

v0:
```python
import jax
import jax.numpy as jnp
from jax import lax
from jax.sharding import PartitionSpec as P

D = 3072
QH = 32
KVH = 8
HD = 128
EXPERTS = 8
EXP_WIN = 1
LEN = 16
BLK = 4
CAP = 8


rope_base = 1000000.0
norm_eps = 1e-05


def shifted(value, axis, steps):
    count = lax.axis_size(axis)
    first, last = (max(0, -steps), min(count, count - steps))
    return lax.ppermute(value, axis, [(source, source + steps) for source in range(first, last)])


def rms_scale(values, gain_vec):
    wide = values.astype(jnp.float32)
    factor = lax.rsqrt(jnp.mean(wide * wide, axis=-1, keepdims=True) + norm_eps)
    return (wide * factor * gain_vec.astype(jnp.float32)).astype(jnp.bfloat16)


def rotate(head_vals, lengths_now):
    half_dim = head_vals.shape[-1] // 2
    inv_freq = rope_base ** (-jnp.arange(half_dim, dtype=jnp.float32) * 2.0 / head_vals.shape[-1])
    angles = lengths_now.astype(jnp.float32)[:, None, None] * inv_freq[None, None, :]
    cosine_vals = jnp.cos(angles)
    sine_table = jnp.sin(angles)
    wide = head_vals.astype(jnp.float32)
    lower_half = wide[..., :half_dim]
    upper_half = wide[..., half_dim:]
    turned = jnp.concatenate(
        [
            lower_half * cosine_vals - upper_half * sine_table,
            upper_half * cosine_vals + lower_half * sine_table,
        ],
        axis=-1,
    )
    return turned.astype(jnp.bfloat16)


def local(
    states,
    entering,
    seq_lens,
    routes,
    attn_norm,
    ffn_norm,
    wq,
    wk,
    wv,
    wo,
    router,
    w_gate,
    w_up,
    w_down,
    cache_k,
    cache_v,
    k_scale,
    v_scale,
):
    ep_size = lax.axis_size("ep")
    ep_index = lax.axis_index("ep")
    section_index = lax.axis_index("section")
    token_rows = states.shape[0]
    heads_here = QH // ep_size
    group_size = QH // KVH
    kv_cols = wk.shape[2]
    q_cols = heads_here * HD
    per_device = q_cols + 2 * kv_cols
    hidden_here = w_gate.shape[2]
    expert_width = hidden_here * ep_size // EXP_WIN
    experts_here = max(1, hidden_here // expert_width)
    ranks_per = max(1, expert_width // hidden_here)
    slot_count = ep_size * experts_here * CAP
    inverse_square_root = HD ** (-0.5)
    joined = jnp.concatenate([wq[0], wk[0], wv[0]], axis=1)
    gate_mat = w_gate[0].reshape(D, experts_here, hidden_here // experts_here)
    up_weight = w_up[0].reshape(D, experts_here, hidden_here // experts_here)
    down_mat = w_down[0].reshape(experts_here, hidden_here // experts_here, D)
    slot_expert = (
        jnp.arange(ep_size, dtype=jnp.int32)[:, None] * experts_here // ranks_per
        + jnp.arange(experts_here, dtype=jnp.int32)[None, :]
    )
    out_matrix = wo[0]

    def run_layer(layer_in, tick_index):
        all_lengths = lax.dynamic_index_in_dim(
            seq_lens, section_index + 1 - tick_index, 0, keepdims=False
        )
        lengths_now = lax.dynamic_slice_in_dim(all_lengths, ep_index * token_rows, token_rows, 0)
        normed = rms_scale(layer_in, attn_norm[0])
        projected = jnp.dot(
            lax.all_gather(normed, "ep", axis=0, tiled=True),
            joined,
            preferred_element_type=jnp.float32,
        ).astype(jnp.bfloat16)
        arrived = lax.all_to_all(projected, "ep", split_axis=0, concat_axis=1, tiled=True).reshape(
            token_rows, ep_size, per_device
        )
        q_all = arrived[:, :, :q_cols].reshape(token_rows, QH, HD)
        fresh_key_rows = rotate(
            arrived[:, :, q_cols : q_cols + kv_cols].reshape(token_rows, KVH, HD), lengths_now
        )
        value_new = arrived[:, :, q_cols + kv_cols :].reshape(token_rows, KVH, HD)
        query_rows = rotate(q_all, lengths_now).reshape(token_rows, KVH, group_size, HD)
        key_codes = cache_k[0, tick_index]
        value_codes = cache_v[0, tick_index]
        key_scales = jnp.repeat(k_scale[0, tick_index], BLK, axis=-1)
        value_scales = jnp.repeat(v_scale[0, tick_index], BLK, axis=-1)
        raw_scores = jnp.einsum(
            "bkgd,bkpd->bkgp", query_rows, key_codes, preferred_element_type=jnp.float32
        )
        scores = raw_scores * key_scales[:, :, None, :] * inverse_square_root
        visible = (jnp.arange(LEN, dtype=jnp.int32)[None, :] < lengths_now[:, None])[
            :, None, None, :
        ]
        current_token_score = (
            jnp.einsum(
                "rwqs,rws->rwq", query_rows, fresh_key_rows, preferred_element_type=jnp.float32
            )
            * inverse_square_root
        )
        row_top = jnp.maximum(
            jnp.max(jnp.where(visible, scores, -1e30), axis=-1), current_token_score
        )
        exponent = jnp.where(visible, jnp.exp(scores - row_top[..., None]), 0.0)
        self_weight = jnp.exp(current_token_score - row_top)
        denom_sum = jnp.sum(exponent, axis=-1) + self_weight
        weights = (exponent * value_scales[:, :, None, :]).astype(jnp.bfloat16)
        mixture = jnp.einsum(
            "bkgp,bkpd->bkgd", weights, value_codes, preferred_element_type=jnp.float32
        )
        mixture = mixture + self_weight[..., None] * value_new.astype(jnp.float32)[:, :, None, :]
        attended = (
            (mixture / denom_sum[..., None]).astype(jnp.bfloat16).reshape(token_rows, QH * HD)
        )
        per_head_split = lax.all_to_all(attended, "ep", split_axis=1, concat_axis=0, tiled=True)
        head_total = lax.psum_scatter(
            jnp.dot(per_head_split, out_matrix, preferred_element_type=jnp.float32),
            "ep",
            scatter_dimension=0,
            tiled=True,
        )
        residual = (layer_in.astype(jnp.float32) + head_total).astype(jnp.bfloat16)
        ffn_input = rms_scale(residual, ffn_norm[0])
        logits = jnp.dot(ffn_input, router[0], preferred_element_type=jnp.float32)
        chosen = routes[0, tick_index]
        hit_table = chosen[:, :, None] == jnp.arange(EXPERTS, dtype=jnp.int32)[None, None, :]
        picked = jnp.sum(jnp.where(hit_table, logits[:, None, :], 0.0), axis=-1)
        gate_probs = jax.nn.softmax(picked, axis=-1)
        earlier = jnp.arange(token_rows)[:, None] > jnp.arange(token_rows)[None, :]
        same_expert = chosen[:, :, None, None] == chosen[None, None, :, :]
        slot_rank = jnp.sum(jnp.where(same_expert & earlier[:, None, :, None], 1, 0), axis=(2, 3))
        matches = (chosen[None, None, None, :, :] == slot_expert[:, :, None, None, None]) & (
            slot_rank[None, None, None]
            == jnp.arange(CAP, dtype=jnp.int32)[None, None, :, None, None]
        )
        selector = jnp.sum(jnp.where(matches, 1.0, 0.0), axis=-1).reshape(slot_count, token_rows)
        gate_table = jnp.sum(
            jnp.where(matches, gate_probs[None, None, None], 0.0), axis=-1
        ).reshape(slot_count, token_rows)
        output_rows = jnp.dot(
            selector.astype(jnp.bfloat16), ffn_input, preferred_element_type=jnp.float32
        ).astype(jnp.bfloat16)
        output_rows = output_rows.reshape(ep_size, experts_here, CAP, D)
        landed = lax.all_to_all(output_rows, "ep", split_axis=0, concat_axis=0, tiled=True)
        gate_act = jnp.einsum(
            "sjcd,djf->sjcf", landed, gate_mat, preferred_element_type=jnp.float32
        )
        up_act = jnp.einsum("sjcd,djf->sjcf", landed, up_weight, preferred_element_type=jnp.float32)
        hidden = (jax.nn.silu(gate_act) * up_act).astype(jnp.bfloat16)
        pieces = jnp.einsum("sjcf,jfd->sjcd", hidden, down_mat, preferred_element_type=jnp.float32)
        returned = lax.all_to_all(pieces, "ep", split_axis=0, concat_axis=0, tiled=True)
        expert_sum = jnp.dot(
            gate_table.T,
            returned.reshape(slot_count, D),
            precision=lax.Precision.HIGHEST,
            preferred_element_type=jnp.float32,
        )
        return (residual.astype(jnp.float32) + expert_sum).astype(jnp.bfloat16)

    first_out = run_layer(states, 0)
    shifted_rows = shifted(first_out, "section", 1)
    second_in = jnp.where(section_index == 0, entering, shifted_rows)
    return run_layer(second_in, 1)


def solution(mesh):
    return jax.shard_map(
        local,
        mesh=mesh,
        in_specs=(
            P(("section", "ep"), None),
            P("ep", None),
            P(),
            P("section", None, "ep", None),
            P("section", None),
            P("section", None),
            P("section", None, "ep"),
            P("section", None, "ep"),
            P("section", None, "ep"),
            P("section", "ep", None),
            P("section", None, None),
            P("section", None, "ep"),
            P("section", None, "ep"),
            P("section", "ep", None),
            P("section", None, "ep", None, None, None),
            P("section", None, "ep", None, None, None),
            P("section", None, "ep", None, None),
            P("section", None, "ep", None, None),
        ),
        out_specs=P(("section", "ep"), None),
        check_vma=False,
    )
```

profile of v0, /device:TPU:0, one launch (start us, length us, event | category | flops | bytes accessed | tf_op | source)
XLA Modules:
  0.0 227.1 jit_solution(4832695848822566199)
XLA Ops:
  7.3 1.0 fusion.92
  8.3 1.0 fusion.94
  9.3 11.0 %all_gather.6 = bf16[64,3072]{1,0:T(8,128)(2,1)S(1)} all-gather(bf16[16,3072]{1,0:T(8,128)(2,1)S(1)} %fusion.94), channel_id=1, replica_groups=mesh['section'=8,'ep'=4] {'ep'}, dimensions={0}, use_global_device_ids=true | all-gather | bytes 491520 | tf_op jit(solution)/shard_map/all_gather | solution.py:104
  20.3 5.5 %fusion.30 = bf16[64,1536]{1,0:T(8,128)(2,1)} fusion(bf16[64,3072]{1,0:T(8,128)(2,1)S(1)} %all_gather.6, bf16[3072,256]{1,0:T(8,128)(2,1)} %bitcast.265, bf16[3072,256]{1,0:T(8,128)(2,1)} %bitcast.267, bf16[3072,1024]{1,0:T(8,128)(2,1)} %bitcast.263), kind=kOutput, calls=%fused_computation.31 | convolution fusion | flops 632389632 | bytes 10027008 | tf_op jit(solution)/shard_map/dot_general | solution.py:103
  25.9 3.5 %all-to-all-start = ((bf16[4,16,1536]{2,1,0:T(8,128)(2,1)}), bf16[4,16,1536]{2,1,0:T(8,128)(2,1)S(1)}, u32[]{:S(2)}, u32[]{:S(2)}) async-start(bf16[4,16,1536]{2,1,0:T(8,128)(2,1)} %bitcast.5), calls=%async_computation | async-start | bytes 393216 | tf_op jit(solution)/shard_map/all_to_all | solution.py:108
  29.8 0.8 fusion.156
  30.9 3.7 %all-to-all-done = bf16[4,16,1536]{2,1,0:T(8,128)(2,1)S(1)} async-done(((bf16[4,16,1536]{2,1,0:T(8,128)(2,1)}), bf16[4,16,1536]{2,1,0:T(8,128)(2,1)S(1)}, u32[]{:S(2)}, u32[]{:S(2)}) %all-to-all-start) | async-done | bytes 196640 | tf_op jit(solution)/shard_map/all_to_all | solution.py:108
  37.4 7.4 %all_to_all.90 = bf16[16,4,1024]{2,0,1:T(8,128)(2,1)S(1)} all-to-all(bf16[16,4,1024]{2,0,1:T(8,128)(2,1)S(1)} %copy.92), channel_id=1, replica_groups=mesh['section'=8,'ep'=4] {'ep'}, dimensions={1} | all-to-all | bytes 262144 | tf_op jit(solution)/shard_map/all_to_all | solution.py:148
  44.8 4.9 %fusion.14 = f32[64,3072]{1,0:T(8,128)} fusion(bf16[64,1024]{1,0:T(8,128)(2,1)S(1)} %bitcast.239, bf16[1,1024,3072]{2,1,0:T(8,128)(2,1)} %param.27), kind=kOutput, calls=%fused_computation.15 | convolution fusion | flops 402653184 | bytes 7208960 | tf_op jit(solution)/shard_map/dot_general | solution.py:150
  50.1 25.6 %reduce-scatter.3.cloned.1.call-done = f32[16,3072]{1,0:T(8,128)} async-done(((f32[64,3072]{1,0:T(8,128)}), f32[16,3072]{1,0:T(8,128)}) %reduce-scatter.3.cloned.1.call-update) | async-done | bytes 196624 | tf_op jit(solution)/shard_map/reduce_scatter | solution.py:149
  75.7 1.1 fusion.96
  77.4 8.1 %all_to_all.91 = bf16[4,1,8,3072]{3,2,1,0:T(8,128)(2,1)S(1)} all-to-all(bf16[4,1,8,3072]{3,2,1,0:T(8,128)(2,1)S(1)} %fusion.24), channel_id=1, replica_groups=mesh['section'=8,'ep'=4] {'ep'}, dimensions={0} | all-to-all | bytes 393216 | tf_op jit(solution)/shard_map/all_to_all | solution.py:177
  85.5 6.0 %fusion.32 = f32[4,1,8,1792]{3,2,0,1:T(8,128)S(1)} fusion(bf16[1,3072,1792]{2,1,0:T(8,128)(2,1)} %param.29, bf16[4,1,8,3072]{3,2,1,0:T(8,128)(2,1)S(1)} %all_to_all.91), kind=kOutput, calls=%fused_computation.33 | convolution fusion | flops 352321536 | bytes 11436032 | tf_op jit(solution)/shard_map/sjcd,djf->sjcf/dot_general | solution.py:178
  91.5 10.9 %fusion.18 = f32[4,1,8,3072]{3,2,1,0:T(8,128)S(1)} fusion(bf16[1,1792,3072]{2,1,0:T(8,128)(2,1)} %param.31, bf16[1,3072,1792]{2,1,0:T(8,128)(2,1)} %param.30, f32[4,1,8,1792]{3,2,0,1:T(8,128)S(1)} %fusion.32, bf16[4,1,8,3072]{3,2,1,0:T(8,128)(2,1)S(1)} %all_to_all.91), kind=kOutput, calls=%fused_computation.19 | convolution fusion | flops 704987136 | bytes 22839296 | tf_op jit(solution)/shard_map/sjcf,jfd->sjcd/dot_general | solution.py:183
  102.4 8.8 %all_to_all.92 = f32[4,1,8,3072]{3,2,1,0:T(8,128)S(1)} all-to-all(f32[4,1,8,3072]{3,2,1,0:T(8,128)S(1)} %fusion.18), channel_id=1, replica_groups=mesh['section'=8,'ep'=4] {'ep'}, dimensions={0} | all-to-all | bytes 786432 | tf_op jit(solution)/shard_map/all_to_all | solution.py:184
  111.6 1.3 collective-permute-start
  112.9 0.9 collective-permute-done
  114.1 8.9 %all_gather.7 = bf16[64,3072]{1,0:T(8,128)(2,1)S(1)} all-gather(bf16[16,3072]{1,0:T(8,128)(2,1)S(1)} %fusion.101), channel_id=1, replica_groups=mesh['section'=8,'ep'=4] {'ep'}, dimensions={0}, use_global_device_ids=true | all-gather | bytes 491520 | tf_op jit(solution)/shard_map/all_gather | solution.py:104
  123.0 5.6 %fusion.31 = bf16[64,1536]{1,0:T(8,128)(2,1)} fusion(bf16[64,3072]{1,0:T(8,128)(2,1)S(1)} %all_gather.7, bf16[3072,256]{1,0:T(8,128)(2,1)S(1)} %bitcast.266, bf16[3072,256]{1,0:T(8,128)(2,1)} %bitcast.268, bf16[3072,1024]{1,0:T(8,128)(2,1)} %bitcast.264), kind=kOutput, calls=%fused_computation.32 | convolution fusion | flops 632389632 | bytes 10027008 | tf_op jit(solution)/shard_map/dot_general | solution.py:103
  128.6 3.4 %all-to-all-start.4 = ((bf16[4,16,1536]{2,1,0:T(8,128)(2,1)}), bf16[4,16,1536]{2,1,0:T(8,128)(2,1)S(1)}, u32[]{:S(2)}, u32[]{:S(2)}) async-start(bf16[4,16,1536]{2,1,0:T(8,128)(2,1)} %bitcast.50), calls=%async_computation.5 | async-start | bytes 393216 | tf_op jit(solution)/shard_map/all_to_all | solution.py:108
  132.5 5.3 %all-to-all-done.4 = bf16[4,16,1536]{2,1,0:T(8,128)(2,1)S(1)} async-done(((bf16[4,16,1536]{2,1,0:T(8,128)(2,1)}), bf16[4,16,1536]{2,1,0:T(8,128)(2,1)S(1)}, u32[]{:S(2)}, u32[]{:S(2)}) %all-to-all-start.4) | async-done | bytes 196640 | tf_op jit(solution)/shard_map/all_to_all | solution.py:108
  138.9 1.6 select_reduce_fusion
  141.0 1.6 fusion.66
  142.7 7.6 %all_to_all.93 = bf16[16,4,1024]{2,0,1:T(8,128)(2,1)S(1)} all-to-all(bf16[16,4,1024]{2,0,1:T(8,128)(2,1)S(1)} %copy.102), channel_id=1, replica_groups=mesh['section'=8,'ep'=4] {'ep'}, dimensions={1} | all-to-all | bytes 262144 | tf_op jit(solution)/shard_map/all_to_all | solution.py:148
  150.3 4.9 %fusion.12 = f32[64,3072]{1,0:T(8,128)} fusion(bf16[64,1024]{1,0:T(8,128)(2,1)S(1)} %bitcast.240, bf16[1,1024,3072]{2,1,0:T(8,128)(2,1)} %param.27), kind=kOutput, calls=%fused_computation.13 | convolution fusion | flops 402653184 | bytes 7208960 | tf_op jit(solution)/shard_map/dot_general | solution.py:150
  155.2 28.7 %reduce-scatter.5.cloned.1.call-done = f32[16,3072]{1,0:T(8,128)} async-done(((f32[64,3072]{1,0:T(8,128)}), f32[16,3072]{1,0:T(8,128)}) %reduce-scatter.5.cloned.1.call-update) | async-done | bytes 196624 | tf_op jit(solution)/shard_map/reduce_scatter | solution.py:149
  183.9 1.1 fusion.103
  185.5 8.1 %all_to_all.94 = bf16[4,1,8,3072]{3,2,1,0:T(8,128)(2,1)S(1)} all-to-all(bf16[4,1,8,3072]{3,2,1,0:T(8,128)(2,1)S(1)} %fusion.25), channel_id=1, replica_groups=mesh['section'=8,'ep'=4] {'ep'}, dimensions={0} | all-to-all | bytes 393216 | tf_op jit(solution)/shard_map/all_to_all | solution.py:177
  193.6 6.0 %fusion.35 = f32[4,1,8,1792]{3,2,0,1:T(8,128)S(1)} fusion(bf16[1,3072,1792]{2,1,0:T(8,128)(2,1)} %param.29, bf16[4,1,8,3072]{3,2,1,0:T(8,128)(2,1)S(1)} %all_to_all.94), kind=kOutput, calls=%fused_computation.34 | convolution fusion | flops 352321536 | bytes 11436032 | tf_op jit(solution)/shard_map/sjcd,djf->sjcf/dot_general | solution.py:178
  199.6 10.8 %fusion.21 = f32[4,1,8,3072]{3,2,1,0:T(8,128)S(1)} fusion(bf16[1,1792,3072]{2,1,0:T(8,128)(2,1)} %param.31, bf16[1,3072,1792]{2,1,0:T(8,128)(2,1)} %param.30, f32[4,1,8,1792]{3,2,0,1:T(8,128)S(1)} %fusion.35, bf16[4,1,8,3072]{3,2,1,0:T(8,128)(2,1)S(1)} %all_to_all.94), kind=kOutput, calls=%fused_computation.20 | convolution fusion | flops 704987136 | bytes 22839296 | tf_op jit(solution)/shard_map/sjcf,jfd->sjcd/dot_general | solution.py:183
  210.4 8.8 %all_to_all.95 = f32[4,1,8,3072]{3,2,1,0:T(8,128)S(1)} all-to-all(f32[4,1,8,3072]{3,2,1,0:T(8,128)S(1)} %fusion.21), channel_id=1, replica_groups=mesh['section'=8,'ep'=4] {'ep'}, dimensions={0} | all-to-all | bytes 786432 | tf_op jit(solution)/shard_map/all_to_all | solution.py:184
  219.2 1.0 fusion.29
  (106 shorter events, 8.2 us)
Async XLA Ops:
  6.5 70.3 %copy-start = (bf16[1,3072,8]{1,2,0:T(8,128)(2,1)S(1)}, bf16[1,3072,8]{1,2,0:T(8,128)(2,1)}, u32[]{:S(2)}) copy-start(bf16[1,3072,8]{1,2,0:T(8,128)(2,1)} %param.28) | copy-start | bytes 147460
  20.3 9.2 %copy-start.3 = (f32[1,2,16,8,4]{2,4,3,1,0:T(4,128)S(1)}, f32[1,2,16,8,4]{2,4,3,1,0:T(4,128)}, u32[]{:S(2)}) copy-start(f32[1,2,16,8,4]{2,4,3,1,0:T(4,128)} %param.34) | copy-start | bytes 12292
  20.3 9.3 %copy-start.4 = (f32[1,2,16,8,4]{2,4,3,1,0:T(4,128)S(1)}, f32[1,2,16,8,4]{2,4,3,1,0:T(4,128)}, u32[]{:S(2)}) copy-start(f32[1,2,16,8,4]{2,4,3,1,0:T(4,128)} %param.35) | copy-start | bytes 12292
  20.3 15.4 %copy-start.8 = (bf16[1,2,16,8,16,128]{5,4,3,2,1,0:T(8,128)(2,1)S(1)}, bf16[1,2,16,8,16,128]{5,4,3,2,1,0:T(8,128)(2,1)}, u32[]{:S(2)}) copy-start(bf16[1,2,16,8,16,128]{5,4,3,2,1,0:T(8,128)(2,1)} %param.32) | copy-start | bytes 3145732
  20.3 16.5 %copy-start.9 = (bf16[1,2,16,8,16,128]{5,4,3,2,1,0:T(8,128)(2,1)S(1)}, bf16[1,2,16,8,16,128]{5,4,3,2,1,0:T(8,128)(2,1)}, u32[]{:S(2)}) copy-start(bf16[1,2,16,8,16,128]{5,4,3,2,1,0:T(8,128)(2,1)} %param.33) | copy-start | bytes 3145732
  25.9 23.8 %copy-start.5 = (bf16[1,3072]{1,0:T(2,128)(2,1)S(1)}, bf16[1,3072]{1,0:T(2,128)(2,1)}, u32[]{:S(2)}) copy-start(bf16[1,3072]{1,0:T(2,128)(2,1)} %param.23) | copy-start | bytes 18436
  25.9 23.9 %copy-start.6 = (s32[1,2,16,2]{2,3,1,0:T(2,128)S(1)}, s32[1,2,16,2]{2,3,1,0:T(2,128)}, u32[]{:S(2)}) copy-start(s32[1,2,16,2]{2,3,1,0:T(2,128)} %param.21) | copy-start | bytes 772
  25.9 49.8 %copy-start.1 = (bf16[16,3072]{1,0:T(8,128)(2,1)S(1)}, bf16[16,3072]{1,0:T(8,128)(2,1)}, u32[]{:S(2)}) copy-start(bf16[16,3072]{1,0:T(8,128)(2,1)} %param.18) | copy-start | bytes 294916
  25.9 8.7 %all-to-all-start = ((bf16[4,16,1536]{2,1,0:T(8,128)(2,1)}), bf16[4,16,1536]{2,1,0:T(8,128)(2,1)S(1)}, u32[]{:S(2)}, u32[]{:S(2)}) async-start(bf16[4,16,1536]{2,1,0:T(8,128)(2,1)} %bitcast.5), calls=%async_computation | async-start | bytes 393216 | tf_op jit(solution)/shard_map/all_to_all | solution.py:108
  29.4 46.3 %reduce-scatter.3.cloned.1.call-start = ((), (), s32[]{:S(2)}) async-start(), calls=%async_computation.10 | async-start | bytes 983040 | tf_op jit(solution)/shard_map/reduce_scatter | solution.py:149
  91.5 22.4 %copy-start.2 = (bf16[16,3072]{1,0:T(8,128)(2,1)S(1)}, bf16[16,3072]{1,0:T(8,128)(2,1)}, u32[]{:S(2)}) copy-start(bf16[16,3072]{1,0:T(8,128)(2,1)} %param.19) | copy-start | bytes 294916
  91.5 31.6 %copy-start.7 = (bf16[1,3072,256]{2,1,0:T(8,128)(2,1)S(1)}, bf16[1,3072,256]{2,1,0:T(8,128)(2,1)}, u32[]{:S(2)}) copy-start(bf16[1,3072,256]{2,1,0:T(8,128)(2,1)} %param.26) | copy-start | bytes 4718596
  111.6 2.2 collective-permute-start
  128.6 9.1 %all-to-all-start.4 = ((bf16[4,16,1536]{2,1,0:T(8,128)(2,1)}), bf16[4,16,1536]{2,1,0:T(8,128)(2,1)S(1)}, u32[]{:S(2)}, u32[]{:S(2)}) async-start(bf16[4,16,1536]{2,1,0:T(8,128)(2,1)} %bitcast.50), calls=%async_computation.5 | async-start | bytes 393216 | tf_op jit(solution)/shard_map/all_to_all | solution.py:108
  132.0 51.9 %reduce-scatter.5.cloned.1.call-start = ((), (), s32[]{:S(2)}) async-start(), calls=%async_computation.11 | async-start | bytes 983040 | tf_op jit(solution)/shard_map/reduce_scatter | solution.py:149
Sparse Core Ops, SparseCore 0:
  49.8 25.8 reduce-scatter.2
  155.3 28.5 reduce-scatter.4
where the time goes:
time: 228 us; the launch traced here: 227 us
  blocking collectives  68.7 us (30%)
  waiting for transfers between devices  64.2 us (28%)
  matrix products  61.8 us (27%)
  between operations  14 us (6%)
  starting transfers between devices  8.43 us (4%)
  other arithmetic  8.32 us (4%)
    reduce_scatter x2, waiting for transfers between devices, run_layer(): lax.psum_scatter(jnp.dot(per_head_split, out_matrix, preferred_element_ty...  54.3 us
    dot_general x2, matrix products, run_layer(): jnp.einsum('sjcf,jfd->sjcd', hidden, down_mat, preferred_element_type=jnp...  21.7 us
    all_gather x2, blocking collectives, run_layer(): lax.all_gather(normed, 'ep', axis=0, tiled=True)  19.9 us
    all_to_all x2, blocking collectives, run_layer(): lax.all_to_all(pieces, 'ep', split_axis=0, concat_axis=0, tiled=True)  17.6 us
    all_to_all x2, blocking collectives, run_layer(): lax.all_to_all(output_rows, 'ep', split_axis=0, concat_axis=0, tiled=True)  16.2 us
    all_to_all x2, blocking collectives, run_layer(): lax.all_to_all(attended, 'ep', split_axis=1, concat_axis=0, tiled=True)  15 us
    dot_general x2, matrix products, run_layer(): jnp.einsum('sjcd,djf->sjcf', landed, gate_mat, preferred_element_type=jnp...  12 us
    dot_general x2, matrix products, run_layer(): jnp.dot(lax.all_gather(normed, 'ep', axis=0, tiled=True), joined, preferr...  11.1 us
  transfers between devices with their start and end apart: 5, of which 5 were waited for; matrix products, arithmetic and copies ran while one was open for 1% of the time, Pallas kernels for 0%

commit v1 on v0

v1 whole, which is shorter than its diff:
```python
import functools

import jax
import jax.numpy as jnp
from jax import lax
from jax.experimental import pallas as pl
from jax.experimental.pallas import tpu as pltpu
from jax.sharding import PartitionSpec as P

QH = 32
KVH = 8
HD = 128
EXPERTS = 8
LEN = 16
BLK = 4
GROUP = QH // KVH
TICKS = 2
PHASES = 6

rope_base = 1000000.0
norm_eps = 1e-05
F32 = jnp.float32
BF16 = jnp.bfloat16
MESH = pl.DeviceIdType.MESH


def rms_scale(values, gain_vec):
    wide = values.astype(F32)
    factor = lax.rsqrt(jnp.mean(wide * wide, axis=-1, keepdims=True) + norm_eps)
    return (wide * factor * gain_vec.astype(F32)).astype(BF16)


def tile_of(columns):
    for tile in (256, 128):
        if columns % tile == 0:
            return tile
    return columns


def over_columns(columns, body):
    tile = tile_of(columns)
    count = columns // tile
    if count == 1:
        body(slice(0, columns), tile)
        return

    @pl.loop(0, count)
    def _(i):
        body(pl.ds(pl.multiple_of(i * tile, tile), tile), tile)


def kernel(
    ep,
    sections,
    states,
    entering,
    attn_gain,
    ffn_gain,
    router,
    cache_k,
    cache_v,
    cos_t,
    sin_t,
    ks_t,
    vs_t,
    bias_t,
    hits_t,
    wq_h,
    wk_h,
    wv_h,
    wo_h,
    wg_h,
    wu_h,
    wd_h,
    out,
    wq,
    wk,
    wv,
    wo,
    wg,
    wu,
    wd,
    x_in,
    y_send,
    shift_recv,
    n_all,
    qkv_send,
    qkv_all,
    att_send,
    att_all,
    wo_send,
    wo_all,
    f_all,
    hidden,
    d_send,
    d_all,
    wsem,
    send_sem,
    recv_sem,
    shift_sem,
):
    me = lax.axis_index("ep")
    sec = lax.axis_index("section")
    rows, width = states.shape
    total = ep * rows
    q_cols = wq.shape[1]
    kv_cols = wk.shape[1]
    heads_here = q_cols // HD
    inv_root = HD ** (-0.5)

    loads = [
        pltpu.make_async_copy(src.at[0], dst, wsem.at[i])
        for i, (src, dst) in enumerate(
            [(wq_h, wq), (wk_h, wk), (wv_h, wv), (wo_h, wo), (wg_h, wg), (wu_h, wu), (wd_h, wd)]
        )
    ]
    for load in loads:
        load.start()

    barrier = pltpu.get_barrier_semaphore()
    for off in range(1, ep):
        pl.semaphore_signal(
            barrier, inc=1, device_id={"ep": lax.rem(me + off, ep)}, device_id_type=MESH
        )
    for off in (1, sections - 1):
        pl.semaphore_signal(
            barrier, inc=1, device_id={"section": lax.rem(sec + off, sections)}, device_id_type=MESH
        )
    x_in[0] = states[...]
    n_all[0, me] = rms_scale(states[...], attn_gain[...])
    pl.semaphore_wait(barrier, ep + 1)

    def exchange(tick, phase, source, target):
        copies = []
        for off in range(1, ep):
            peer = lax.rem(me + off, ep)
            copies.append(
                pltpu.make_async_remote_copy(
                    src_ref=source(peer),
                    dst_ref=target.at[tick, me],
                    send_sem=send_sem.at[tick * PHASES + phase, off - 1],
                    recv_sem=recv_sem.at[tick * PHASES + phase, off - 1],
                    device_id={"ep": peer},
                    device_id_type=MESH,
                )
            )
        for copy in copies:
            copy.start()
        return copies

    def finish(copies):
        for copy in copies:
            copy.wait()

    def split(values):
        return values.reshape(ep, rows, values.shape[-1])

    for tick in range(TICKS):
        x = x_in[tick]
        if tick:
            n_all[tick, me] = rms_scale(x, attn_gain[...])
        finish(exchange(tick, 0, lambda peer: n_all.at[tick, me], n_all))

        def project(weight, base):
            def body(cols, tile):
                got = jnp.dot(
                    n_all[tick].reshape(total, width), weight[:, cols], preferred_element_type=F32
                )
                if isinstance(cols, slice):
                    place = slice(base, base + tile)
                else:
                    place = pl.ds(pl.multiple_of(cols.start + base, tile), tile)
                qkv_send[tick, :, :, place] = split(got.astype(BF16))

            over_columns(weight.shape[1], body)

        for i, (weight, base) in enumerate(((wq, 0), (wk, q_cols), (wv, q_cols + kv_cols))):
            if tick == 0:
                loads[i].wait()
            project(weight, base)
        copies = exchange(tick, 1, lambda peer: qkv_send.at[tick, peer], qkv_all)
        qkv_all[tick, me] = qkv_send[tick, me]
        finish(copies)

        cos_v, sin_v = cos_t[tick], sin_t[tick]

        def turn(head):
            return (head * cos_v + pltpu.roll(head, HD // 2, 1) * sin_v).astype(BF16)

        def q_head(h):
            at = (h % heads_here) * HD
            return qkv_all[tick, h // heads_here, :, at : at + HD].astype(F32)

        def kv_head(base, k):
            if kv_cols >= HD:
                per = kv_cols // HD
                at = base + (k % per) * HD
                return qkv_all[tick, k // per, :, at : at + HD].astype(F32)
            per = HD // kv_cols
            return jnp.concatenate(
                [
                    qkv_all[tick, k * per + i, :, base : base + kv_cols].astype(F32)
                    for i in range(per)
                ],
                axis=-1,
            )

        for k in range(KVH):
            queries = jnp.concatenate([turn(q_head(k * GROUP + g)) for g in range(GROUP)], axis=0)
            key_new = turn(kv_head(q_cols, k)).astype(F32)
            value_new = kv_head(q_cols + kv_cols, k)
            key_codes = cache_k[0, tick, :, k].reshape(rows * LEN, HD)
            value_codes = cache_v[0, tick, :, k].reshape(rows * LEN, HD)
            raw = lax.dot_general(
                queries, key_codes, (((1,), (1,)), ((), ())), preferred_element_type=F32
            )
            scores = raw * ks_t[tick, k : k + 1] * inv_root + bias_t[tick]
            own = (
                jnp.sum(
                    queries.astype(F32) * jnp.concatenate([key_new] * GROUP, axis=0),
                    axis=-1,
                    keepdims=True,
                )
                * inv_root
            )
            top = jnp.maximum(jnp.max(scores, axis=-1, keepdims=True), own)
            exponent = jnp.exp(scores - top)
            self_weight = jnp.exp(own - top)
            denom = jnp.sum(exponent, axis=-1, keepdims=True) + self_weight
            weights = (exponent * vs_t[tick, k : k + 1]).astype(BF16)
            mixture = jnp.dot(weights, value_codes, preferred_element_type=F32)
            mixture = mixture + self_weight * jnp.concatenate([value_new] * GROUP, axis=0)
            attended = (mixture / denom).astype(BF16)
            for g in range(GROUP):
                h = k * GROUP + g
                at = (h % heads_here) * HD
                att_send[tick, h // heads_here, :, at : at + HD] = attended[
                    g * rows : (g + 1) * rows
                ]
        copies = exchange(tick, 2, lambda peer: att_send.at[tick, peer], att_all)
        att_all[tick, me] = att_send[tick, me]
        finish(copies)

        if tick == 0:
            loads[3].wait()

        def out_body(cols, tile):
            got = jnp.dot(
                att_all[tick].reshape(total, q_cols), wo[:, cols], preferred_element_type=F32
            )
            wo_send[tick, :, :, cols] = split(got.astype(BF16))

        over_columns(width, out_body)
        copies = exchange(tick, 3, lambda peer: wo_send.at[tick, peer], wo_all)
        wo_all[tick, me] = wo_send[tick, me]
        finish(copies)
        head_total = jnp.sum(wo_all[tick].astype(F32), axis=0)
        residual = (x_in[tick].astype(F32) + head_total).astype(BF16)
        ffn_input = rms_scale(residual, ffn_gain[...])
        f_all[tick, me] = ffn_input
        copies = exchange(tick, 4, lambda peer: f_all.at[tick, me], f_all)
        logits = jnp.dot(ffn_input, router[0], preferred_element_type=F32)
        first, second = hits_t[tick, 0], hits_t[tick, 1]
        pick_a = jnp.sum(logits * first, axis=-1, keepdims=True)
        pick_b = jnp.sum(logits * second, axis=-1, keepdims=True)
        best = jnp.maximum(pick_a, pick_b)
        exp_a, exp_b = jnp.exp(pick_a - best), jnp.exp(pick_b - best)
        share = (exp_a * first[:, :1] + exp_b * second[:, :1]) / (exp_a + exp_b)
        finish(copies)

        if tick == 0:
            loads[4].wait()
            loads[5].wait()

        def up_body(cols, tile):
            landed = f_all[tick].reshape(total, width)
            gate = jnp.dot(landed, wg[:, cols], preferred_element_type=F32)
            up = jnp.dot(landed, wu[:, cols], preferred_element_type=F32)
            hidden[:, cols] = (gate / (1.0 + jnp.exp(-gate)) * up).astype(BF16)

        over_columns(wg.shape[1], up_body)
        if tick == 0:
            loads[6].wait()

        def down_body(cols, tile):
            got = jnp.dot(hidden[...], wd[:, cols], preferred_element_type=F32)
            d_send[tick, :, :, cols] = split(got.astype(BF16))

        over_columns(width, down_body)
        copies = exchange(tick, 5, lambda peer: d_send.at[tick, peer], d_all)
        d_all[tick, me] = d_send[tick, me]
        finish(copies)
        expert_sum = jnp.sum(d_all[tick].astype(F32), axis=0) * share
        result = (residual.astype(F32) + expert_sum).astype(BF16)
        if tick == TICKS - 1:
            out[...] = result
        else:
            y_send[...] = result
            shift = pltpu.make_async_remote_copy(
                src_ref=y_send,
                dst_ref=shift_recv,
                send_sem=shift_sem.at[0],
                recv_sem=shift_sem.at[1],
                device_id={"section": lax.rem(sec + 1, sections)},
                device_id_type=MESH,
            )

            @pl.when(sec < sections - 1)
            def _():
                shift.start()

            @pl.when(sec == 0)
            def _():
                x_in[1] = entering[...]

            @pl.when(sec > 0)
            def _():
                shift.wait_recv()
                x_in[1] = shift_recv[...]

            @pl.when(sec < sections - 1)
            def _():
                shift.wait_send()


def local(
    states,
    entering,
    seq_lens,
    routes,
    attn_norm,
    ffn_norm,
    wq,
    wk,
    wv,
    wo,
    router,
    w_gate,
    w_up,
    w_down,
    cache_k,
    cache_v,
    k_scale,
    v_scale,
):
    ep = lax.axis_size("ep")
    sections = lax.axis_size("section")
    me = lax.axis_index("ep")
    sec = lax.axis_index("section")
    rows, width = states.shape
    q_cols, kv_cols, units = wq.shape[2], wk.shape[2], w_gate.shape[2]
    per_device = q_cols + 2 * kv_cols

    lengths = jnp.stack(
        [
            lax.dynamic_slice(seq_lens, (sec + 1 - tick, me * rows), (1, rows))[0]
            for tick in range(TICKS)
        ]
    )
    half = HD // 2
    inv_freq = rope_base ** (-jnp.arange(half, dtype=F32) * 2.0 / HD)
    angles = lengths.astype(F32)[:, :, None] * inv_freq[None, None, :]
    cos, sin = jnp.cos(angles), jnp.sin(angles)
    cos_t = jnp.concatenate([cos, cos], axis=-1)
    sin_t = jnp.concatenate([-sin, sin], axis=-1)

    def spread(scale):
        wide = jnp.repeat(scale[0], BLK, axis=-1)
        return wide.transpose(0, 2, 1, 3).reshape(TICKS, KVH, rows * LEN)

    place = jnp.arange(rows * LEN, dtype=jnp.int32)
    live = (place % LEN)[None, :] < jnp.repeat(lengths, LEN, axis=-1)
    same = (jnp.arange(GROUP * rows, dtype=jnp.int32) % rows)[:, None] == (place // LEN)[None, :]
    bias_t = jnp.where(same[None] & live[:, None, :], 0.0, -1e30).astype(F32)
    chosen = routes[0].transpose(0, 2, 1)
    hits_t = (chosen[..., None] == jnp.arange(EXPERTS, dtype=jnp.int32)).astype(F32)

    vmem = pl.BlockSpec(memory_space=pltpu.VMEM)
    anyspace = pl.BlockSpec(memory_space=pl.ANY)

    def buf(*shape):
        return pltpu.VMEM(shape, BF16)

    return pl.pallas_call(
        functools.partial(kernel, ep, sections),
        out_shape=jax.ShapeDtypeStruct((rows, width), BF16),
        in_specs=[vmem] * 13 + [anyspace] * 7,
        out_specs=vmem,
        scratch_shapes=[
            buf(width, q_cols),
            buf(width, kv_cols),
            buf(width, kv_cols),
            buf(q_cols, width),
            buf(width, units),
            buf(width, units),
            buf(units, width),
            buf(TICKS, rows, width),
            buf(rows, width),
            buf(rows, width),
            buf(TICKS, ep, rows, width),
            buf(TICKS, ep, rows, per_device),
            buf(TICKS, ep, rows, per_device),
            buf(TICKS, ep, rows, q_cols),
            buf(TICKS, ep, rows, q_cols),
            buf(TICKS, ep, rows, width),
            buf(TICKS, ep, rows, width),
            buf(TICKS, ep, rows, width),
            buf(ep * rows, units),
            buf(TICKS, ep, rows, width),
            buf(TICKS, ep, rows, width),
            pltpu.SemaphoreType.DMA((7,)),
            pltpu.SemaphoreType.DMA((TICKS * PHASES, ep - 1)),
            pltpu.SemaphoreType.DMA((TICKS * PHASES, ep - 1)),
            pltpu.SemaphoreType.DMA((2,)),
        ],
        compiler_params=pltpu.CompilerParams(
            collective_id=0, has_side_effects=True, vmem_limit_bytes=67043328
        ),
        name="decode_window",
    )(
        states,
        entering,
        attn_norm,
        ffn_norm,
        router,
        cache_k,
        cache_v,
        cos_t,
        sin_t,
        spread(k_scale),
        spread(v_scale),
        bias_t,
        hits_t,
        wq,
        wk,
        wv,
        wo,
        w_gate,
        w_up,
        w_down,
    )


def solution(mesh):
    return jax.shard_map(
        local,
        mesh=mesh,
        in_specs=(
            P(("section", "ep"), None),
            P("ep", None),
            P(),
            P("section", None, "ep", None),
            P("section", None),
            P("section", None),
            P("section", None, "ep"),
            P("section", None, "ep"),
            P("section", None, "ep"),
            P("section", "ep", None),
            P("section", None, None),
            P("section", None, "ep"),
            P("section", None, "ep"),
            P("section", "ep", None),
            P("section", None, "ep", None, None, None),
            P("section", None, "ep", None, None, None),
            P("section", None, "ep", None, None),
            P("section", None, "ep", None, None),
        ),
        out_specs=P(("section", "ep"), None),
        check_vma=False,
    )
```

time: 228 us -> 112 us (0.49)
  Pallas kernels: 0 us -> 101 us
  blocking collectives: 68.7 us -> 0 us
  waiting for transfers between devices: 64.2 us -> 0 us
  matrix products: 61.8 us -> 0 us
  between operations: 14 us -> 0.07 us
  starting transfers between devices: 8.43 us -> 0 us
  local copies, waits for them, and re-layouts: 1.5 us -> 7.67 us
  other arithmetic: 8.32 us -> 2.98 us
    pallas_call x0 -> x1, Pallas kernels: none -> 101 us  [local(): pl.pallas_call(functools.partial(kernel, ep, sections), out_shape=jax.Sha...]
    dot_general x20 -> x0, matrix products: 61.8 us -> none  [the longest x2 21.7 us: run_layer(): jnp.einsum('sjcf,jfd->sjcd', hidden, down_mat, preferred_element_type=jnp...]
    reduce_scatter x2 -> x0, waiting for transfers between devices: 54.3 us -> none  [run_layer(): lax.psum_scatter(jnp.dot(per_head_split, out_matrix, preferred_element_ty...]
    all_to_all x6 -> x0, blocking collectives: 48.8 us -> none  [the longest x2 17.6 us: run_layer(): lax.all_to_all(pieces, 'ep', split_axis=0, concat_axis=0, tiled=True)]
    all_gather x2 -> x0, blocking collectives: 19.9 us -> none  [run_layer(): lax.all_gather(normed, 'ep', axis=0, tiled=True)]
    all_to_all x2 -> x0, waiting for transfers between devices: 8.99 us -> none  [run_layer(): lax.all_to_all(projected, 'ep', split_axis=0, concat_axis=1, tiled=True)]
    all_to_all x2 -> x0, starting transfers between devices: 6.87 us -> none  [run_layer(): lax.all_to_all(projected, 'ep', split_axis=0, concat_axis=1, tiled=True)]
    reduce_sum x13 -> x0, other arithmetic: 4.46 us -> none  [the longest x4 3.32 us: rms_scale(): factor = lax.rsqrt(jnp.mean(wide * wide, axis=-1, keepdims=True) + norm_eps)]
  transfers between devices with their start and end apart: 5 -> 0, of which waited for: 5 -> 0; matrix products, arithmetic and copies ran while one was open for 1% -> 0% of each run, Pallas kernels for 0% -> 0%
where the time goes in v1:
time: 112 us
  Pallas kernels  101 us (90%)
  local copies, waits for them, and re-layouts  7.67 us (7%)
  other arithmetic  2.98 us (3%)
    pallas_call x1, Pallas kernels, local(): pl.pallas_call(functools.partial(kernel, ep, sections), out_shape=jax.Sha...  101 us
    unnamed x2, local copies, waits for them, and re-layouts  3.5 us

profile of v1, /device:TPU:0, one launch (start us, length us, event | category | flops | bytes accessed | tf_op | source)
XLA Modules:
  0.0 111.7 jit_solution(5626493762985537299)
XLA Ops:
  0.0 0.8 fusion.5
  0.9 0.1 broadcast_compare_fusion
  1.0 0.1 broadcast_in_dim.28
  1.1 0.1 reshape.115
  1.1 1.4 %fusion.hits_t = f32[2,2,16,8]{3,2,1,0:T(8,128)} fusion(s32[2,2,16]{2,1,0:T(2,128)} %bitcast.19), kind=kLoop, calls=%fused_computation.3 | loop fusion | flops 1024 | bytes 2304 | tf_op jit(solution)/shard_map/convert_element_type | solution.py:376
  2.5 0.8 copy.22
  3.3 0.8 copy.24
  4.0 0.1 fusion.1
  4.2 0.7 pad_maximum_fusion
  4.9 0.1 copy.25
  5.0 0.7 reshape.114.vs_t
  5.7 0.1 copy.23
  5.8 0.7 reshape.112.ks_t
  6.5 0.7 and_select_fusion.bias_t
  7.2 2.0 %copy.26.router = bf16[1,3072,8]{2,1,0:T(8,128)(2,1)} copy(bf16[1,3072,8]{1,2,0:T(8,128)(2,1)} %param.28) | data formatting | bytes 98304 | tf_op args[10]
  9.2 101.0 %decode_window.1 = bf16[16,3072]{1,0:T(8,128)(2,1)} custom-call(bf16[16,3072]{1,0:T(8,128)(2,1)} %states.1, bf16[16,3072]{1,0:T(8,128)(2,1)} %entering.1, bf16[1,3072]{1,0:T(2,128)(2,1)} %attn_gain.1, bf16[1,3072]{1,0:T(2,128)(2,1)} %ffn_gain.1, bf16[1,3072,8]{2,1,0:T(8,128)(2,1)} %copy.26.router, bf16[1,2,16,8,16,128]{5,4,3,2,1,0:T(8,128)(2,1)} %cache_k.1, ...), custom_call_target="tpu_custom_call" | custom-call | tf_op jit(solution)/shard_map/decode_window/pallas_call | solution.py:384
  110.2 1.5 %copy.28 = bf16[16,3072]{1,0:T(8,128)(2,1)} copy(bf16[16,3072]{1,0:T(8,128)(2,1)} %decode_window.1) | data formatting | bytes 196608
  (8 shorter events, 0.1 us)
